TPU v7x, 32 devices: a whole 2x2x4 slice. The times are simulated.
32 devices in a mesh: row: 4 (over z), col: 8 (over y, x, core).
Axes of the slice: x: 2, y: 2, z: 4, core: 2. Of those that a mesh axis runs over, the one named last changes fastest.
Arguments:
- residual: float32 [8192, 2048], P('row', 'col'), may hold values from -6 to 6
- point_spread: float32 [1024, 1024], P('col'), may hold values from -0.6 to 1
- peak_pixels: int32 [4, 64, 2], replicated, may hold values from 0 to 8191, as said below
Outputs:
- cleaned: float32 [8192, 2048], P('row', 'col')
- tile_peak: float32 [4, 8], P('row', 'col')
- components: float32 [4, 64], replicated
Inputs may be any that keep to these rules, and one draw needn't show every extreme that they name: peak_pixels[r, k, 0] is a row below 8192 and peak_pixels[r, k, 1] a column below 2048; positions may repeat.
All inputs are finite; a program needn't handle non-finite values.
Results may differ from a plain program's by a relative error of at most 0.00002.
Values sent between devices are 32-bit elements; how exact they have to be, the bound alone decides.
No kernel may reach another device: no remote copies, remote signals or barrier semaphores. Data moves between devices by JAX's collectives and lax.ppermute only.
A program may use at most 64 MiB of HBM per device.

v0:
```python
import jax
import jax.numpy as jnp
from jax import lax
from jax.sharding import PartitionSpec as P

loop_gain = 0.1


def subtract_rows(buffer, widened, row_offset, col_start, amplitudes, ordering, active):
    rows_here = widened.shape[0]
    tile_cols = buffer.shape[1]

    def remove_one(position, current):
        chosen = ordering[position]
        first_row = row_offset[chosen]
        window = lax.dynamic_slice(
            widened, (jnp.int32(0), col_start[chosen]), (rows_here, tile_cols)
        )
        before = lax.dynamic_slice(current, (first_row, jnp.int32(0)), (rows_here, tile_cols))
        return lax.dynamic_update_slice(
            current, before - amplitudes[chosen] * window, (first_row, jnp.int32(0))
        )

    return lax.fori_loop(0, active, remove_one, buffer)


def own_values(buffer, peak_rows, peak_cols, row_base, col_base, tile_rows, tile_cols, extent):
    local_rows = peak_rows - row_base
    local_cols = peak_cols - col_base
    owning = (
        (local_rows >= 0) & (local_rows < tile_rows) & (local_cols >= 0) & (local_cols < tile_cols)
    )
    picked = buffer[
        jnp.clip(local_rows, 0, tile_rows - 1) + extent, jnp.clip(local_cols, 0, tile_cols - 1)
    ]
    return jnp.where(owning, picked, 0.0)


def round_values(buffer, peak_rows, peak_cols, row_base, col_base, tile_rows, tile_cols, extent):
    partial_value = own_values(
        buffer, peak_rows, peak_cols, row_base, col_base, tile_rows, tile_cols, extent
    )
    return lax.psum(partial_value, ("row", "col"))


def local(residual, point_spread, peak_pixels):
    tile_rows, tile_cols = residual.shape
    extent = point_spread.shape[1]
    half_width = extent // 2
    rounds = peak_pixels.shape[0]
    row_base = lax.axis_index("row") * tile_rows
    col_base = lax.axis_index("col") * tile_cols
    buffer = jnp.pad(residual, ((extent, extent), (0, 0)))
    peak_rows = peak_pixels[:, :, 0]
    peak_cols = peak_pixels[:, :, 1]
    row_offset = peak_rows - row_base + half_width
    col_start = col_base - peak_cols + half_width + tile_cols
    inside = (
        (row_offset > 0)
        & (row_offset < tile_rows + extent)
        & (col_start > 0)
        & (col_start < extent + tile_cols)
    )
    ordering = jnp.argsort(jnp.where(inside, 0, 1).astype(jnp.int32), axis=1, stable=True)
    counts = jnp.sum(inside.astype(jnp.int32), axis=1)
    amplitudes = loop_gain * round_values(
        buffer, peak_rows[0], peak_cols[0], row_base, col_base, tile_rows, tile_cols, extent
    )
    assembled = lax.all_gather(point_spread, "col", axis=0, tiled=True)
    widened = jnp.pad(assembled, ((0, 0), (tile_cols, tile_cols)))
    buffer = subtract_rows(
        buffer, widened, row_offset[0], col_start[0], amplitudes, ordering[0], counts[0]
    )
    amplitude_rows = [amplitudes]
    for round_index in range(1, rounds):
        amplitudes = loop_gain * round_values(
            buffer,
            peak_rows[round_index],
            peak_cols[round_index],
            row_base,
            col_base,
            tile_rows,
            tile_cols,
            extent,
        )
        buffer = subtract_rows(
            buffer,
            widened,
            row_offset[round_index],
            col_start[round_index],
            amplitudes,
            ordering[round_index],
            counts[round_index],
        )
        amplitude_rows.append(amplitudes)
    cleaned = buffer[extent : extent + tile_rows]
    tile_peak = jnp.max(jnp.abs(cleaned)).reshape(1, 1)
    return (cleaned, tile_peak, jnp.stack(amplitude_rows))


def solution(mesh):
    return jax.shard_map(
        local,
        mesh=mesh,
        in_specs=(P("row", "col"), P("col", None), P()),
        out_specs=(P("row", "col"), P("row", "col"), P()),
        check_vma=False,
    )
```

profile of v0, /device:TPU:29, one launch (start us, length us, event | category | flops | bytes accessed | tf_op | source)
XLA Modules:
  0.0 1655.7 jit_solution(7925653327540661939)
XLA Ops:
  8.8 3.9 pad.8
  16.5 38.2 %psum.28 = f32[64]{0:T(128)S(1)} all-reduce(f32[64]{0:T(128)S(1)} %bitcast_select_fusion.3), channel_id=1, replica_groups=mesh['row'=4,'col'=8] {'row','col'}, use_global_device_ids=true, to_apply=%region_2.3 | all-reduce | flops 64 | bytes 512 | tf_op jit(solution)/shard_map/psum | solution.py:43
  55.8 5.7 pad.9
  61.5 130.2 %while.40 = (s32[]{:T(128)}, f32[4096,256]{1,0:T(8,128)}, s32[]{:T(128)}, s32[64]{0:T(128)S(1)}, s32[64]{0:T(128)S(1)}, /*index=5*/f32[64]{0:T(128)S(1)}, s32[64...) while((s32[]{:T(128)}, f32[4096,256]{1,0:T(8,128)}, ...), condition=%wide.region_4.5_spmd, body=%wide.region_3.4_spmd.sunk | while | flops 524302 | bytes 5243205 | solution.py:24
  73.5 4.1 dynamic_update_slice.16
  89.7 4.1 dynamic_update_slice.16
  105.9 4.1 dynamic_update_slice.16
  122.1 4.1 dynamic_update_slice.16
  138.3 4.1 dynamic_update_slice.16
  154.5 4.1 dynamic_update_slice.16
  170.7 4.1 dynamic_update_slice.16
  186.8 4.1 dynamic_update_slice.16
  194.6 312.5 %psum.29 = f32[64]{0:T(128)S(1)} all-reduce(f32[64]{0:T(128)S(1)} %bitcast_select_fusion.2), channel_id=1, replica_groups=mesh['row'=4,'col'=8] {'row','col'}, use_global_device_ids=true, to_apply=%region_5.6 | all-reduce | flops 64 | bytes 512 | tf_op jit(solution)/shard_map/psum | solution.py:43
  507.1 146.5 %while.41 = (s32[]{:T(128)}, f32[4096,256]{1,0:T(8,128)}, s32[]{:T(128)}, s32[64]{0:T(128)S(1)}, s32[64]{0:T(128)S(1)}, /*index=5*/f32[64]{0:T(128)S(1)}, s32[64...) while((s32[]{:T(128)}, f32[4096,256]{1,0:T(8,128)}, ...), condition=%wide.region_7.8_spmd, body=%wide.region_6.7_spmd.sunk | while | flops 524302 | bytes 5243205 | solution.py:24
  519.1 4.1 dynamic_update_slice.17
  535.3 4.1 dynamic_update_slice.17
  551.5 4.1 dynamic_update_slice.17
  567.7 4.1 dynamic_update_slice.17
  583.9 4.1 dynamic_update_slice.17
  600.2 4.1 dynamic_update_slice.17
  616.4 4.1 dynamic_update_slice.17
  632.6 4.1 dynamic_update_slice.17
  648.8 4.1 dynamic_update_slice.17
  656.3 280.8 %psum.30 = f32[64]{0:T(128)S(1)} all-reduce(f32[64]{0:T(128)S(1)} %bitcast_select_fusion.1), channel_id=1, replica_groups=mesh['row'=4,'col'=8] {'row','col'}, use_global_device_ids=true, to_apply=%region_8.9 | all-reduce | flops 64 | bytes 512 | tf_op jit(solution)/shard_map/psum | solution.py:43
  937.1 210.4 %while.42 = (s32[]{:T(128)}, f32[4096,256]{1,0:T(8,128)}, s32[]{:T(128)}, s32[64]{0:T(128)S(1)}, s32[64]{0:T(128)S(1)}, /*index=5*/f32[64]{0:T(128)S(1)}, s32[64...) while((s32[]{:T(128)}, f32[4096,256]{1,0:T(8,128)}, ...), condition=%wide.region_10.11_spmd, body=%wide.region_9.10_spmd.sunk | while | flops 524302 | bytes 5243205 | solution.py:24
  949.2 4.1 dynamic_update_slice.18
  965.3 4.1 dynamic_update_slice.18
  981.4 4.1 dynamic_update_slice.18
  997.6 4.1 dynamic_update_slice.18
  1013.7 4.1 dynamic_update_slice.18
  1029.8 4.1 dynamic_update_slice.18
  1046.0 4.1 dynamic_update_slice.18
  1062.2 4.1 dynamic_update_slice.18
  1078.3 4.1 dynamic_update_slice.18
  1094.4 4.1 dynamic_update_slice.18
  1110.5 4.1 dynamic_update_slice.18
  1126.7 4.1 dynamic_update_slice.18
  1142.8 4.1 dynamic_update_slice.18
  1150.0 117.7 %psum.31 = f32[64]{0:T(128)S(1)} all-reduce(f32[64]{0:T(128)S(1)} %bitcast_select_fusion), channel_id=1, replica_groups=mesh['row'=4,'col'=8] {'row','col'}, use_global_device_ids=true, to_apply=%region_11.12 | all-reduce | flops 64 | bytes 512 | tf_op jit(solution)/shard_map/psum | solution.py:43
  1267.7 376.8 %while.43 = (s32[]{:T(128)}, f32[4096,256]{1,0:T(8,128)}, s32[]{:T(128)}, s32[64]{0:T(128)S(1)}, s32[64]{0:T(128)S(1)}, /*index=5*/f32[64]{0:T(128)S(1)}, s32[64...) while((s32[]{:T(128)}, f32[4096,256]{1,0:T(8,128)}, ...), condition=%wide.region_13.14_spmd, body=%wide.region_12.13_spmd.sunk | while | flops 524302 | bytes 5243205 | solution.py:24
  1279.2 4.1 dynamic_update_slice.19
  1294.9 4.2 dynamic_update_slice.19
  1310.6 4.1 dynamic_update_slice.19
  1326.3 4.1 dynamic_update_slice.19
  1341.9 4.1 dynamic_update_slice.19
  1357.6 4.1 dynamic_update_slice.19
  1373.3 4.2 dynamic_update_slice.19
  1389.0 4.1 dynamic_update_slice.19
  1404.7 4.1 dynamic_update_slice.19
  1420.3 4.1 dynamic_update_slice.19
  1436.0 4.1 dynamic_update_slice.19
  1451.7 4.1 dynamic_update_slice.19
  1467.3 4.1 dynamic_update_slice.19
  1483.0 4.1 dynamic_update_slice.19
  1498.6 4.1 dynamic_update_slice.19
  1514.3 4.1 dynamic_update_slice.19
  1530.0 4.1 dynamic_update_slice.19
  1545.6 4.1 dynamic_update_slice.19
  1561.3 4.1 dynamic_update_slice.19
  1577.1 4.1 dynamic_update_slice.19
  1592.7 4.1 dynamic_update_slice.19
  1608.4 4.1 dynamic_update_slice.19
  1624.1 4.1 dynamic_update_slice.19
  1639.7 4.1 dynamic_update_slice.19
  (299 shorter events, 299.9 us)
Async XLA Ops:
  7.2 5.5 copy-start
  7.2 48.6 %all-gather.2.cloned.1.call-start = ((), (), s32[]{:S(2)}) async-start(), calls=%async_computation | async-start | bytes 4718592 | tf_op jit(solution)/shard_map/all_gather | solution.py:69
Sparse Core Ops, SparseCore 0:
  9.9 38.3 all-gather.1
where the time goes:
time: 1670 us; the launch traced here: 1660 us
  blocking collectives  749 us (45%)
  local copies, waits for them, and re-layouts  378 us (23%)
  loops' own time  361 us (22%)
  other arithmetic  152 us (9%)
    psum x4, blocking collectives, round_values(): return lax.psum(partial_value, ('row', 'col'))  749 us
    another operation x4, loops' own time, subtract_rows(): return lax.fori_loop(0, active, remove_one, buffer)  361 us
    dynamic_update_slice x54, local copies, waits for them, and re-layouts, remove_one(): lax.dynamic_update_slice(current, before - amplitudes[chosen] * window, (...  222 us
    sub x54, other arithmetic, remove_one(): before - amplitudes[chosen] * window  147 us
    dynamic_slice x54, local copies, waits for them, and re-layouts, remove_one(): col_start[chosen]  33.6 us
    dynamic_slice x54, local copies, waits for them, and re-layouts, remove_one(): amplitudes[chosen] * window  33.6 us
    dynamic_slice x54, local copies, waits for them, and re-layouts, remove_one(): chosen = ordering[position]  33.5 us
    dynamic_slice x54, local copies, waits for them, and re-layouts, remove_one(): first_row = row_offset[chosen]  33.5 us
  transfers between devices with their start and end apart: 1, of which 0 were waited for; matrix products, arithmetic and copies ran while one was open for 1% of the time, Pallas kernels for 0%

commit v1 on v0

--- a/solution.py
+++ b/solution.py
@@ -4,6 +4,11 @@
 from jax.sharding import PartitionSpec as P
 
 loop_gain = 0.1
+
+
+def gather_and_add(array, axis):
+    parts = lax.all_gather(array, axis)
+    return jnp.sum(parts, axis=0)
 
 
 def subtract_rows(buffer, widened, row_offset, col_start, amplitudes, ordering, active):
@@ -40,7 +45,7 @@
     partial_value = own_values(
         buffer, peak_rows, peak_cols, row_base, col_base, tile_rows, tile_cols, extent
     )
-    return lax.psum(partial_value, ("row", "col"))
+    return gather_and_add(partial_value, ("row", "col"))
 
 
 def local(residual, point_spread, peak_pixels):

time: 1670 us -> 1630 us (0.976)
  blocking collectives: 749 us -> 712 us
    psum x4 -> x0, blocking collectives: 749 us -> none  [round_values(): return lax.psum(partial_value, ('row', 'col'))]
    all_gather x0 -> x4, blocking collectives: none -> 712 us  [gather_and_add(): parts = lax.all_gather(array, axis)]
where the time goes in v1:
time: 1630 us; the launch traced here: 1620 us
  blocking collectives  712 us (44%)
  local copies, waits for them, and re-layouts  378 us (23%)
  loops' own time  361 us (22%)
  other arithmetic  153 us (9%)
    all_gather x4, blocking collectives, gather_and_add(): parts = lax.all_gather(array, axis)  712 us
    another operation x4, loops' own time, subtract_rows(): return lax.fori_loop(0, active, remove_one, buffer)  361 us
    dynamic_update_slice x54, local copies, waits for them, and re-layouts, remove_one(): lax.dynamic_update_slice(current, before - amplitudes[chosen] * window, (...  222 us
    sub x54, other arithmetic, remove_one(): before - amplitudes[chosen] * window  147 us
    dynamic_slice x54, local copies, waits for them, and re-layouts, remove_one(): amplitudes[chosen] * window  33.6 us
    dynamic_slice x54, local copies, waits for them, and re-layouts, remove_one(): col_start[chosen]  33.6 us
    dynamic_slice x54, local copies, waits for them, and re-layouts, remove_one(): first_row = row_offset[chosen]  33.5 us
    dynamic_slice x54, local copies, waits for them, and re-layouts, remove_one(): chosen = ordering[position]  33.5 us
  transfers between devices with their start and end apart: 1, of which 0 were waited for; matrix products, arithmetic and copies ran while one was open for 1% of the time, Pallas kernels for 0%

profile of v1, /device:TPU:29, one launch (start us, length us, event | category | flops | bytes accessed | tf_op | source)
XLA Modules:
  0.0 1618.0 jit_solution(7974321947657330470)
XLA Ops:
  7.9 3.9 pad.8
  14.6 36.1 %all-gather = f32[32,1,64]{2,1,0:T(1,128)S(1)} all-gather(f32[1,1,64]{2,1,0:T(1,128)S(1)} %fusion.20), channel_id=1, replica_groups=mesh['row'=4,'col'=8] {'row','col'}, dimensions={0}, use_global_device_ids=true | all-gather | bytes 8448 | tf_op jit(solution)/shard_map/all_gather | solution.py:10
  53.0 5.7 pad.9
  58.7 130.2 %while.40 = (s32[]{:T(128)}, f32[4096,256]{1,0:T(8,128)}, s32[]{:T(128)}, s32[64]{0:T(128)S(1)}, s32[64]{0:T(128)S(1)}, /*index=5*/f32[64]{0:T(128)S(1)}, s32[64...) while((s32[]{:T(128)}, f32[4096,256]{1,0:T(8,128)}, ...), condition=%wide.region_4.5_spmd, body=%wide.region_3.4_spmd.sunk | while | flops 524302 | bytes 5243205 | solution.py:29
  70.8 4.1 dynamic_update_slice.16
  87.0 4.1 dynamic_update_slice.16
  103.1 4.1 dynamic_update_slice.16
  119.3 4.1 dynamic_update_slice.16
  135.5 4.1 dynamic_update_slice.16
  151.7 4.1 dynamic_update_slice.16
  167.9 4.1 dynamic_update_slice.16
  184.1 4.1 dynamic_update_slice.16
  191.8 295.1 %all-gather.1 = f32[32,1,64]{2,1,0:T(1,128)S(1)} all-gather(f32[1,1,64]{2,1,0:T(1,128)S(1)} %fusion.21), channel_id=1, replica_groups=mesh['row'=4,'col'=8] {'row','col'}, dimensions={0}, use_global_device_ids=true | all-gather | bytes 8448 | tf_op jit(solution)/shard_map/all_gather | solution.py:10
  487.0 146.5 %while.41 = (s32[]{:T(128)}, f32[4096,256]{1,0:T(8,128)}, s32[]{:T(128)}, s32[64]{0:T(128)S(1)}, s32[64]{0:T(128)S(1)}, /*index=5*/f32[64]{0:T(128)S(1)}, s32[64...) while((s32[]{:T(128)}, f32[4096,256]{1,0:T(8,128)}, ...), condition=%wide.region_7.8_spmd, body=%wide.region_6.7_spmd.sunk | while | flops 524302 | bytes 5243205 | solution.py:29
  499.1 4.1 dynamic_update_slice.17
  515.3 4.1 dynamic_update_slice.17
  531.5 4.1 dynamic_update_slice.17
  547.7 4.1 dynamic_update_slice.17
  563.9 4.1 dynamic_update_slice.17
  580.2 4.1 dynamic_update_slice.17
  596.3 4.1 dynamic_update_slice.17
  612.5 4.1 dynamic_update_slice.17
  628.7 4.1 dynamic_update_slice.17
  636.2 279.3 %all-gather.2 = f32[32,1,64]{2,1,0:T(1,128)S(1)} all-gather(f32[1,1,64]{2,1,0:T(1,128)S(1)} %fusion.22), channel_id=1, replica_groups=mesh['row'=4,'col'=8] {'row','col'}, dimensions={0}, use_global_device_ids=true | all-gather | bytes 8448 | tf_op jit(solution)/shard_map/all_gather | solution.py:10
  915.6 210.4 %while.42 = (s32[]{:T(128)}, f32[4096,256]{1,0:T(8,128)}, s32[]{:T(128)}, s32[64]{0:T(128)S(1)}, s32[64]{0:T(128)S(1)}, /*index=5*/f32[64]{0:T(128)S(1)}, s32[64...) while((s32[]{:T(128)}, f32[4096,256]{1,0:T(8,128)}, ...), condition=%wide.region_10.11_spmd, body=%wide.region_9.10_spmd.sunk | while | flops 524302 | bytes 5243205 | solution.py:29
  927.6 4.1 dynamic_update_slice.18
  943.7 4.1 dynamic_update_slice.18
  959.9 4.1 dynamic_update_slice.18
  976.0 4.1 dynamic_update_slice.18
  992.2 4.1 dynamic_update_slice.18
  1008.3 4.1 dynamic_update_slice.18
  1024.4 4.1 dynamic_update_slice.18
  1040.6 4.1 dynamic_update_slice.18
  1056.7 4.1 dynamic_update_slice.18
  1072.9 4.1 dynamic_update_slice.18
  1089.0 4.1 dynamic_update_slice.18
  1105.1 4.1 dynamic_update_slice.18
  1121.3 4.1 dynamic_update_slice.18
  1128.4 101.5 %all-gather.3 = f32[32,1,64]{2,1,0:T(1,128)S(1)} all-gather(f32[1,1,64]{2,1,0:T(1,128)S(1)} %fusion.23), channel_id=1, replica_groups=mesh['row'=4,'col'=8] {'row','col'}, dimensions={0}, use_global_device_ids=true | all-gather | bytes 8448 | tf_op jit(solution)/shard_map/all_gather | solution.py:10
  1230.0 376.9 %while.43 = (s32[]{:T(128)}, f32[4096,256]{1,0:T(8,128)}, s32[]{:T(128)}, s32[64]{0:T(128)S(1)}, s32[64]{0:T(128)S(1)}, /*index=5*/f32[64]{0:T(128)S(1)}, s32[64...) while((s32[]{:T(128)}, f32[4096,256]{1,0:T(8,128)}, ...), condition=%wide.region_13.14_spmd, body=%wide.region_12.13_spmd.sunk | while | flops 524302 | bytes 5243205 | solution.py:29
  1241.6 4.1 dynamic_update_slice.19
  1257.2 4.2 dynamic_update_slice.19
  1272.9 4.1 dynamic_update_slice.19
  1288.6 4.1 dynamic_update_slice.19
  1304.3 4.1 dynamic_update_slice.19
  1320.0 4.1 dynamic_update_slice.19
  1335.6 4.2 dynamic_update_slice.19
  1351.4 4.1 dynamic_update_slice.19
  1367.0 4.1 dynamic_update_slice.19
  1382.7 4.1 dynamic_update_slice.19
  1398.4 4.1 dynamic_update_slice.19
  1414.0 4.1 dynamic_update_slice.19
  1429.7 4.1 dynamic_update_slice.19
  1445.3 4.1 dynamic_update_slice.19
  1461.0 4.1 dynamic_update_slice.19
  1476.7 4.1 dynamic_update_slice.19
  1492.3 4.1 dynamic_update_slice.19
  1508.0 4.1 dynamic_update_slice.19
  1523.7 4.1 dynamic_update_slice.19
  1539.5 4.1 dynamic_update_slice.19
  1555.1 4.1 dynamic_update_slice.19
  1570.8 4.1 dynamic_update_slice.19
  1586.5 4.1 dynamic_update_slice.19
  1602.1 4.1 dynamic_update_slice.19
  (303 shorter events, 299.3 us)
Async XLA Ops:
  7.2 4.7 copy-start
  7.2 45.8 %all-gather.6.cloned.1.call-start = ((), (), s32[]{:S(2)}) async-start(), calls=%async_computation | async-start | bytes 4718592 | tf_op jit(solution)/shard_map/all_gather | solution.py:74
Sparse Core Ops, SparseCore 0:
  9.9 37.8 all-gather.5

commit v2 on v0

--- a/solution.py
+++ b/solution.py
@@ -4,6 +4,11 @@
 from jax.sharding import PartitionSpec as P
 
 loop_gain = 0.1
+
+
+def by_each_axis(x, axis_one, axis_two):
+    partial = lax.psum(x, axis_one)
+    return lax.psum(partial, axis_two)
 
 
 def subtract_rows(buffer, widened, row_offset, col_start, amplitudes, ordering, active):
@@ -40,7 +45,7 @@
     partial_value = own_values(
         buffer, peak_rows, peak_cols, row_base, col_base, tile_rows, tile_cols, extent
     )
-    return lax.psum(partial_value, ("row", "col"))
+    return by_each_axis(partial_value, "row", "col")
 
 
 def local(residual, point_spread, peak_pixels):

time: 1670 us -> 1610 us (0.964)
  blocking collectives: 749 us -> 673 us
    psum x4 -> x8, blocking collectives: 749 us -> 673 us  [the longest x4 349 us: by_each_axis(): partial = lax.psum(x, axis_one)]
  transfers between devices with their start and end apart: 1 -> 1, of which waited for: 0 -> 1; matrix products, arithmetic and copies ran while one was open for 1% -> 1% of each run, Pallas kernels for 0% -> 0%
where the time goes in v2:
time: 1610 us; the launch traced here: 1590 us
  blocking collectives  673 us (42%)
  local copies, waits for them, and re-layouts  378 us (23%)
  loops' own time  361 us (22%)
  other arithmetic  152 us (9%)
    another operation x4, loops' own time, subtract_rows(): return lax.fori_loop(0, active, remove_one, buffer)  361 us
    psum x4, blocking collectives, by_each_axis(): partial = lax.psum(x, axis_one)  349 us
    psum x4, blocking collectives, by_each_axis(): return lax.psum(partial, axis_two)  324 us
    dynamic_update_slice x54, local copies, waits for them, and re-layouts, remove_one(): lax.dynamic_update_slice(current, before - amplitudes[chosen] * window, (...  222 us
    sub x54, other arithmetic, remove_one(): before - amplitudes[chosen] * window  147 us
    dynamic_slice x54, local copies, waits for them, and re-layouts, remove_one(): amplitudes[chosen] * window  33.6 us
    dynamic_slice x54, local copies, waits for them, and re-layouts, remove_one(): col_start[chosen]  33.6 us
    dynamic_slice x54, local copies, waits for them, and re-layouts, remove_one(): chosen = ordering[position]  33.5 us
  transfers between devices with their start and end apart: 1, of which 1 were waited for; matrix products, arithmetic and copies ran while one was open for 1% of the time, Pallas kernels for 0%

profile of v2, /device:TPU:29, one launch (start us, length us, event | category | flops | bytes accessed | tf_op | source)
XLA Modules:
  0.0 1589.9 jit_solution(9138083974829281676)
XLA Ops:
  16.5 6.4 psum.56
  22.9 13.4 psum.57
  37.3 10.4 all-gather.2.cloned.1.call-done
  47.7 5.7 pad.9
  53.4 130.2 %while.40 = (s32[]{:T(128)}, f32[4096,256]{1,0:T(8,128)}, s32[]{:T(128)}, s32[64]{0:T(128)S(1)}, s32[64]{0:T(128)S(1)}, /*index=5*/f32[64]{0:T(128)S(1)}, s32[64...) while((s32[]{:T(128)}, f32[4096,256]{1,0:T(8,128)}, ...), condition=%wide.region_5.6_spmd, body=%wide.region_4.5_spmd.sunk | while | flops 524302 | bytes 5243205 | solution.py:29
  65.5 4.1 dynamic_update_slice.16
  81.7 4.1 dynamic_update_slice.16
  97.9 4.1 dynamic_update_slice.16
  114.1 4.1 dynamic_update_slice.16
  130.3 4.1 dynamic_update_slice.16
  146.5 4.1 dynamic_update_slice.16
  178.8 4.1 dynamic_update_slice.16
  186.6 246.4 %psum.58 = f32[64]{0:T(128)S(1)} all-reduce(f32[64]{0:T(128)S(1)} %bitcast_select_fusion.2), channel_id=1, replica_groups=mesh['row'=4,'col'=8] {'row'}, use_global_device_ids=true, to_apply=%region_6.7 | all-reduce | flops 64 | bytes 512 | tf_op jit(solution)/shard_map/psum | solution.py:10
  433.0 46.0 %psum.59 = f32[64]{0:T(128)S(1)} all-reduce(f32[64]{0:T(128)S(1)} %psum.58), channel_id=1, replica_groups=mesh['row'=4,'col'=8] {'col'}, use_global_device_ids=true, to_apply=%region_7.8 | all-reduce | flops 64 | bytes 512 | tf_op jit(solution)/shard_map/psum | solution.py:11
  478.9 146.5 %while.41 = (s32[]{:T(128)}, f32[4096,256]{1,0:T(8,128)}, s32[]{:T(128)}, s32[64]{0:T(128)S(1)}, s32[64]{0:T(128)S(1)}, /*index=5*/f32[64]{0:T(128)S(1)}, s32[64...) while((s32[]{:T(128)}, f32[4096,256]{1,0:T(8,128)}, ...), condition=%wide.region_9.10_spmd, body=%wide.region_8.9_spmd.sunk | while | flops 524302 | bytes 5243205 | solution.py:29
  491.0 4.1 dynamic_update_slice.17
  507.2 4.1 dynamic_update_slice.17
  523.4 4.1 dynamic_update_slice.17
  539.6 4.1 dynamic_update_slice.17
  555.8 4.1 dynamic_update_slice.17
  572.1 4.1 dynamic_update_slice.17
  588.3 4.1 dynamic_update_slice.17
  604.5 4.1 dynamic_update_slice.17
  620.7 4.1 dynamic_update_slice.17
  628.2 41.0 %psum.60 = f32[64]{0:T(128)S(1)} all-reduce(f32[64]{0:T(128)S(1)} %bitcast_select_fusion.1), channel_id=1, replica_groups=mesh['row'=4,'col'=8] {'row'}, use_global_device_ids=true, to_apply=%region_10.11 | all-reduce | flops 64 | bytes 512 | tf_op jit(solution)/shard_map/psum | solution.py:10
  669.2 221.1 %psum.61 = f32[64]{0:T(128)S(1)} all-reduce(f32[64]{0:T(128)S(1)} %psum.60), channel_id=1, replica_groups=mesh['row'=4,'col'=8] {'col'}, use_global_device_ids=true, to_apply=%region_11.12 | all-reduce | flops 64 | bytes 512 | tf_op jit(solution)/shard_map/psum | solution.py:11
  890.3 210.4 %while.42 = (s32[]{:T(128)}, f32[4096,256]{1,0:T(8,128)}, s32[]{:T(128)}, s32[64]{0:T(128)S(1)}, s32[64]{0:T(128)S(1)}, /*index=5*/f32[64]{0:T(128)S(1)}, s32[64...) while((s32[]{:T(128)}, f32[4096,256]{1,0:T(8,128)}, ...), condition=%wide.region_13.14_spmd, body=%wide.region_12.13_spmd.sunk | while | flops 524302 | bytes 5243205 | solution.py:29
  902.3 4.1 dynamic_update_slice.18
  918.4 4.1 dynamic_update_slice.18
  950.7 4.1 dynamic_update_slice.18
  966.8 4.1 dynamic_update_slice.18
  983.0 4.1 dynamic_update_slice.18
  1015.3 4.1 dynamic_update_slice.18
  1031.4 4.1 dynamic_update_slice.18
  1047.5 4.1 dynamic_update_slice.18
  1063.7 4.1 dynamic_update_slice.18
  1079.8 4.1 dynamic_update_slice.18
  1096.0 4.1 dynamic_update_slice.18
  1103.1 54.8 %psum.62 = f32[64]{0:T(128)S(1)} all-reduce(f32[64]{0:T(128)S(1)} %bitcast_select_fusion), channel_id=1, replica_groups=mesh['row'=4,'col'=8] {'row'}, use_global_device_ids=true, to_apply=%region_14.15 | all-reduce | flops 64 | bytes 512 | tf_op jit(solution)/shard_map/psum | solution.py:10
  1157.9 44.0 %psum.63 = f32[64]{0:T(128)S(1)} all-reduce(f32[64]{0:T(128)S(1)} %psum.62), channel_id=1, replica_groups=mesh['row'=4,'col'=8] {'col'}, use_global_device_ids=true, to_apply=%region_15.16 | all-reduce | flops 64 | bytes 512 | tf_op jit(solution)/shard_map/psum | solution.py:11
  1201.9 376.9 %while.43 = (s32[]{:T(128)}, f32[4096,256]{1,0:T(8,128)}, s32[]{:T(128)}, s32[64]{0:T(128)S(1)}, s32[64]{0:T(128)S(1)}, /*index=5*/f32[64]{0:T(128)S(1)}, s32[64...) while((s32[]{:T(128)}, f32[4096,256]{1,0:T(8,128)}, ...), condition=%wide.region_17.18_spmd, body=%wide.region_16.17_spmd.sunk | while | flops 524302 | bytes 5243205 | solution.py:29
  1213.5 4.1 dynamic_update_slice.19
  1229.1 4.2 dynamic_update_slice.19
  1244.8 4.1 dynamic_update_slice.19
  1260.5 4.1 dynamic_update_slice.19
  1276.1 4.1 dynamic_update_slice.19
  1291.8 4.1 dynamic_update_slice.19
  1307.5 4.2 dynamic_update_slice.19
  1323.2 4.1 dynamic_update_slice.19
  1338.9 4.1 dynamic_update_slice.19
  1354.6 4.1 dynamic_update_slice.19
  1370.2 4.1 dynamic_update_slice.19
  1385.9 4.1 dynamic_update_slice.19
  1401.6 4.1 dynamic_update_slice.19
  1417.2 4.1 dynamic_update_slice.19
  1432.9 4.1 dynamic_update_slice.19
  1448.5 4.1 dynamic_update_slice.19
  1464.2 4.1 dynamic_update_slice.19
  1479.9 4.1 dynamic_update_slice.19
  1511.3 4.1 dynamic_update_slice.19
  1527.0 4.1 dynamic_update_slice.19
  1542.7 4.1 dynamic_update_slice.19
  1558.3 4.1 dynamic_update_slice.19
  1574.0 4.1 dynamic_update_slice.19
  (303 shorter events, 320.1 us)
Async XLA Ops:
  7.2 5.5 copy-start
  7.2 40.6 %all-gather.2.cloned.1.call-start = ((), (), s32[]{:S(2)}) async-start(), calls=%async_computation | async-start | bytes 4718592 | tf_op jit(solution)/shard_map/all_gather | solution.py:74
Sparse Core Ops, SparseCore 0:
  9.9 37.8 all-gather.1
